TPU v7x, 32 devices: a whole 2x2x4 slice. The times are simulated.
32 devices in a mesh: dp: 8 (over y, x, core), mp: 4 (over z).
Axes of the slice: x: 2, y: 2, z: 4, core: 2. Of those that a mesh axis runs over, the one named last changes fastest.
Arguments:
- tokens: bfloat16 [8192, 2048], P('dp'), may hold values from -6 to 6
- cotangent: bfloat16 [8192, 2048], P('dp'), may hold values from -6 to 6
- counts: int32 [8], replicated, may hold values from 1 to 1024, 5120 in all
- w_qkv: bfloat16 [2048, 3, 2048], P('dp', None, 'mp'), may hold values from -0.125 to 0.125
- w_out: bfloat16 [2048, 2048], P('mp', 'dp'), may hold values from -1 to 1
- w_fc1: bfloat16 [2048, 8192], P('dp', 'mp'), may hold values from -0.125 to 0.125
- w_fc2: bfloat16 [8192, 2048], P('mp', 'dp'), may hold values from -0.0625 to 0.0625
- ln1_gain: bfloat16 [2048], P('dp'), may hold values from 0.5 to 1.5
- ln1_bias: bfloat16 [2048], P('dp'), may hold values from -1.796875 to 1.796875
- ln2_gain: bfloat16 [2048], P('dp'), may hold values from 0.5 to 1.5
- ln2_bias: bfloat16 [2048], P('dp'), may hold values from -1.796875 to 1.796875
- qv_bias: bfloat16 [2, 2048], P(None, ('mp', 'dp')), may hold values from -1.796875 to 1.796875
- out_bias: bfloat16 [2048], P('dp'), may hold values from -1.796875 to 1.796875
- fc1_bias: bfloat16 [8192], P(('mp', 'dp')), may hold values from -1.796875 to 1.796875
- fc2_bias: bfloat16 [2048], P('dp'), may hold values from -1.796875 to 1.796875
Outputs:
- out_tokens: bfloat16 [8192, 2048], P('dp')
- grad_tokens: float32 [8192, 2048], P('dp')
- grad_w_qkv: float32 [2048, 3, 2048], P('dp', None, 'mp')
- grad_w_out: float32 [2048, 2048], P('mp', 'dp')
- grad_w_fc1: float32 [2048, 8192], P('dp', 'mp')
- grad_w_fc2: float32 [8192, 2048], P('mp', 'dp')
- grad_ln1_gain: float32 [2048], P('dp')
- grad_ln1_bias: float32 [2048], P('dp')
- grad_ln2_gain: float32 [2048], P('dp')
- grad_ln2_bias: float32 [2048], P('dp')
- grad_qv_bias: float32 [2, 2048], P(None, ('mp', 'dp'))
- grad_out_bias: float32 [2048], P('dp')
- grad_fc1_bias: float32 [8192], P(('mp', 'dp'))
- grad_fc2_bias: float32 [2048], P('dp')
Inputs may be any that keep to these rules, and one draw needn't show every extreme that they name: counts[g] is the number of live tokens of group g's sequence, at the start of its 1024 slots; the largest count equals 1024.
All inputs are finite; a program needn't handle non-finite values.
Results may differ from a plain program's by a relative error of at most 0.014.
Values may be sent and summed in bfloat16 or wider, within the bound.
A program may use at most 192 MiB of HBM per device.

v0:
```python
import math
import jax
import jax.numpy as jnp
from jax import lax
from jax.sharding import PartitionSpec as P

HEAD = 128
EPS = 1e-05
NEG = -1e30


def layer_norm(values, gain_vec, shift_vec):
    center = values - jnp.mean(values, axis=-1, keepdims=True)
    spread = jnp.mean(center * center, axis=-1, keepdims=True)
    return center * lax.rsqrt(spread + EPS) * gain_vec + shift_vec


def smooth_gate(values):
    return jax.nn.gelu(values, approximate=True)


def causal_scores(queries, key_heads, inv_root):
    row_count = queries.shape[0]
    raw_scores = (
        jnp.einsum("qhd,khd->hqk", queries, key_heads, preferred_element_type=jnp.float32)
        * inv_root
    )
    future = lax.broadcasted_iota(jnp.int32, (row_count, row_count), 1) > lax.broadcasted_iota(
        jnp.int32, (row_count, row_count), 0
    )
    return jnp.where(future[None], NEG, raw_scores)


def shards(
    tokens,
    cotangent,
    counts,
    w_qkv,
    w_out,
    w_fc1,
    w_fc2,
    ln1_gain,
    ln1_bias,
    ln2_gain,
    ln2_bias,
    qv_bias,
    out_bias,
    fc1_bias,
    fc2_bias,
):
    gathered = (
        lax.all_gather(w_qkv, "dp", axis=0, tiled=True),
        lax.all_gather(w_out, "dp", axis=1, tiled=True),
        lax.all_gather(w_fc1, "dp", axis=0, tiled=True),
        lax.all_gather(w_fc2, "dp", axis=1, tiled=True),
        lax.all_gather(ln1_gain, "dp", axis=0, tiled=True),
        lax.all_gather(ln1_bias, "dp", axis=0, tiled=True),
        lax.all_gather(ln2_gain, "dp", axis=0, tiled=True),
        lax.all_gather(ln2_bias, "dp", axis=0, tiled=True),
        lax.all_gather(qv_bias, "dp", axis=1, tiled=True),
        lax.all_gather(out_bias, "dp", axis=0, tiled=True),
        lax.all_gather(fc1_bias, "dp", axis=0, tiled=True),
        lax.all_gather(fc2_bias, "dp", axis=0, tiled=True),
    )
    whole_qkv, whole_out, whole_fc1, whole_fc2 = (
        gathered[0],
        gathered[1],
        gathered[2],
        gathered[3],
    )
    gain_one = gathered[4].astype(jnp.float32)
    shift_one = gathered[5].astype(jnp.float32)
    gain_two = gathered[6].astype(jnp.float32)
    shift_two = gathered[7].astype(jnp.float32)
    bias_qv = gathered[8].astype(jnp.float32)
    bias_out = gathered[9].astype(jnp.float32)
    bias_fc1 = gathered[10].astype(jnp.float32)
    bias_fc2 = gathered[11].astype(jnp.float32)
    seq_rows = tokens.shape[0]
    local_width = whole_qkv.shape[2]
    heads_here = local_width // HEAD
    inv_root = 1.0 / math.sqrt(HEAD)
    inputs = tokens.astype(jnp.float32)
    normed_one = layer_norm(inputs, gain_one, shift_one).astype(jnp.bfloat16)
    projected = jnp.einsum("sd,dce->sce", normed_one, whole_qkv, preferred_element_type=jnp.float32)
    queries = (
        (projected[:, 0] + bias_qv[0]).astype(jnp.bfloat16).reshape(seq_rows, heads_here, HEAD)
    )
    key_heads = projected[:, 1].astype(jnp.bfloat16).reshape(seq_rows, heads_here, HEAD)
    values = (projected[:, 2] + bias_qv[1]).astype(jnp.bfloat16).reshape(seq_rows, heads_here, HEAD)
    scores = causal_scores(queries, key_heads, inv_root)
    row_peak = jnp.max(scores, axis=-1, keepdims=True)
    exp_terms = jnp.exp(scores - row_peak)
    exp_total = jnp.sum(exp_terms, axis=-1, keepdims=True)
    log_total = row_peak + jnp.log(exp_total)
    prob_low = (exp_terms / exp_total).astype(jnp.bfloat16)
    mixed_heads = (
        jnp.einsum("hqk,khd->qhd", prob_low, values, preferred_element_type=jnp.float32)
        .astype(jnp.bfloat16)
        .reshape(seq_rows, local_width)
    )
    attn_part = jnp.dot(mixed_heads, whole_out, preferred_element_type=jnp.float32)
    residual = inputs + lax.psum(attn_part, "mp") + bias_out
    normed_two = layer_norm(residual, gain_two, shift_two).astype(jnp.bfloat16)
    preact = jnp.dot(normed_two, whole_fc1, preferred_element_type=jnp.float32) + bias_fc1
    activated = smooth_gate(preact).astype(jnp.bfloat16)
    ffn_part = jnp.dot(activated, whole_fc2, preferred_element_type=jnp.float32)
    out_tokens = (
        residual + lax.psum(ffn_part.astype(jnp.bfloat16), "mp").astype(jnp.float32) + bias_fc2
    ).astype(jnp.bfloat16)
    dp_index = lax.axis_index("dp")
    slot_ids = lax.iota(jnp.int32, counts.shape[0])
    own_count = jnp.sum(jnp.where(slot_ids == dp_index, counts, 0))
    weight_share = own_count.astype(jnp.float32) / jnp.sum(counts).astype(jnp.float32)
    live_rows = lax.iota(jnp.int32, seq_rows) < own_count
    grad_out = jnp.where(live_rows[:, None], cotangent.astype(jnp.float32), 0.0)
    grad_out_low = grad_out.astype(jnp.bfloat16)
    grad_fc2 = (
        jnp.einsum("sf,sd->fd", activated, grad_out_low, preferred_element_type=jnp.float32)
        * weight_share
    )
    grad_fc2_bias = jnp.sum(grad_out, axis=0) * weight_share
    delta_act = jnp.einsum("sd,fd->sf", grad_out_low, whole_fc2, preferred_element_type=jnp.float32)
    unused_gate, gate_back = jax.vjp(smooth_gate, preact)
    delta_pre = gate_back(delta_act)[0]
    grad_fc1_bias = jnp.sum(delta_pre, axis=0) * weight_share
    delta_pre_low = delta_pre.astype(jnp.bfloat16)
    grad_fc1 = (
        jnp.einsum("sd,sf->df", normed_two, delta_pre_low, preferred_element_type=jnp.float32)
        * weight_share
    )
    two_part = jnp.einsum("sf,df->sd", delta_pre_low, whole_fc1, preferred_element_type=jnp.float32)
    delta_two = lax.psum(two_part, "mp")
    unused_two, second_back = jax.vjp(layer_norm, residual, gain_two, shift_two)
    resid_part, gain_two_part, shift_two_part = second_back(delta_two)
    delta_resid = resid_part + grad_out
    delta_resid_low = delta_resid.astype(jnp.bfloat16)
    out_bias_part = jnp.sum(delta_resid, axis=0)
    grad_out_proj = (
        jnp.einsum("sc,sd->cd", mixed_heads, delta_resid_low, preferred_element_type=jnp.float32)
        * weight_share
    )
    delta_mixed = jnp.einsum(
        "sd,cd->sc", delta_resid_low, whole_out, preferred_element_type=jnp.float32
    )
    delta_mixed_low = delta_mixed.astype(jnp.bfloat16).reshape(seq_rows, heads_here, HEAD)
    scores_again = causal_scores(queries, key_heads, inv_root)
    prob_full = jnp.exp(scores_again - log_total)
    delta_prob = jnp.einsum(
        "qhd,khd->hqk", delta_mixed_low, values, preferred_element_type=jnp.float32
    )
    delta_scores = prob_full * (
        delta_prob - jnp.sum(prob_full * delta_prob, axis=-1, keepdims=True)
    )
    delta_scores_low = delta_scores.astype(jnp.bfloat16)
    delta_q = (
        jnp.einsum("hqk,khd->qhd", delta_scores_low, key_heads, preferred_element_type=jnp.float32)
        * inv_root
    ).reshape(seq_rows, local_width)
    delta_k = (
        jnp.einsum("hqk,qhd->khd", delta_scores_low, queries, preferred_element_type=jnp.float32)
        * inv_root
    ).reshape(seq_rows, local_width)
    delta_v = jnp.einsum(
        "hqk,qhd->khd", prob_low, delta_mixed_low, preferred_element_type=jnp.float32
    ).reshape(seq_rows, local_width)
    grad_qv = jnp.stack([jnp.sum(delta_q, axis=0), jnp.sum(delta_v, axis=0)]) * weight_share
    delta_proj = jnp.stack([delta_q, delta_k, delta_v], axis=1).astype(jnp.bfloat16)
    grad_qkv = (
        jnp.einsum("sd,sce->dce", normed_one, delta_proj, preferred_element_type=jnp.float32)
        * weight_share
    )
    one_part = jnp.einsum("sce,dce->sd", delta_proj, whole_qkv, preferred_element_type=jnp.float32)
    delta_one = lax.psum(one_part.astype(jnp.bfloat16), "mp").astype(jnp.float32)
    unused_one, first_back = jax.vjp(layer_norm, inputs, gain_one, shift_one)
    input_part, gain_one_part, shift_one_part = first_back(delta_one)
    grad_tokens = input_part + delta_resid
    stat_sums = jnp.stack(
        [gain_two_part, shift_two_part, out_bias_part, gain_one_part, shift_one_part]
    )
    stat_weighted = stat_sums * weight_share
    summed_all = (
        lax.psum_scatter(grad_qkv, "dp", scatter_dimension=0, tiled=True),
        lax.psum_scatter(grad_out_proj, "dp", scatter_dimension=1, tiled=True),
        lax.psum_scatter(grad_qv, "dp", scatter_dimension=1, tiled=True),
        lax.psum_scatter(stat_weighted[2], "dp", scatter_dimension=0, tiled=True),
        lax.psum_scatter(stat_weighted[3], "dp", scatter_dimension=0, tiled=True),
        lax.psum_scatter(stat_weighted[4], "dp", scatter_dimension=0, tiled=True),
        lax.psum_scatter(grad_fc1, "dp", scatter_dimension=0, tiled=True),
        lax.psum_scatter(grad_fc2, "dp", scatter_dimension=1, tiled=True),
        lax.psum_scatter(grad_fc1_bias, "dp", scatter_dimension=0, tiled=True),
        lax.psum_scatter(grad_fc2_bias, "dp", scatter_dimension=0, tiled=True),
        lax.psum_scatter(stat_weighted[0], "dp", scatter_dimension=0, tiled=True),
        lax.psum_scatter(stat_weighted[1], "dp", scatter_dimension=0, tiled=True),
    )
    return (
        out_tokens,
        grad_tokens,
        summed_all[0],
        summed_all[1],
        summed_all[6],
        summed_all[7],
        summed_all[4],
        summed_all[5],
        summed_all[10],
        summed_all[11],
        summed_all[2],
        summed_all[3],
        summed_all[8],
        summed_all[9],
    )


def solution(mesh):
    placed = (
        P("dp", None),
        P("dp", None),
        P(),
        P("dp", None, "mp"),
        P("mp", "dp"),
        P("dp", "mp"),
        P("mp", "dp"),
        P("dp"),
        P("dp"),
        P("dp"),
        P("dp"),
        P(None, ("mp", "dp")),
        P("dp"),
        P(("mp", "dp")),
        P("dp"),
    )
    return jax.shard_map(
        shards,
        mesh=mesh,
        in_specs=placed,
        out_specs=(
            P("dp", None),
            P("dp", None),
            P("dp", None, "mp"),
            P("mp", "dp"),
            P("dp", "mp"),
            P("mp", "dp"),
            P("dp"),
            P("dp"),
            P("dp"),
            P("dp"),
            P(None, ("mp", "dp")),
            P("dp"),
            P(("mp", "dp")),
            P("dp"),
        ),
        check_vma=False,
    )
```

profile of v0, /device:TPU:0, one launch (start us, length us, event | category | flops | bytes accessed | tf_op | source)
XLA Modules:
  0.0 1627.1 jit_solution(16595095688366546610)
XLA Ops:
  7.2 2.3 copy.76
  9.6 0.7 all-gather.15.cloned.1.call-update
  12.0 10.4 all-gather.2
  22.4 2.9 convert_reduce_fusion.1
  25.3 3.4 fusion.15
  28.8 8.9 all-gather.1
  37.7 8.6 all-gather
  46.3 13.5 all-gather.13.cloned.1.call-done
  59.8 10.4 fusion.38
  70.4 1.7 fusion.54
  72.1 7.7 fusion.57
  79.8 8.1 fusion
  87.9 2.0 copy.78
  89.9 8.5 divide_convert_fusion
  98.4 3.2 copy-done.2
  101.6 1.4 convolution_convert_fusion.1
  103.1 7.7 fusion.59
  112.2 9.1 all-gather.6
  121.3 8.0 all-gather.3
  129.3 8.9 all-gather.5
  138.2 8.0 all-gather.4
  147.5 254.6 %all-reduce.13.cloned.1.call-done = f32[1024,2048]{1,0:T(8,128)} async-done(((f32[1024,2048]{1,0:T(8,128)}), f32[1024,2048]{1,0:T(8,128)}) %all-reduce.13.cloned.1.call-update) | async-done | bytes 8388624 | tf_op jit(solution)/shard_map/psum | solution.py:103
  402.1 5.7 fusion.52
  407.8 3.5 copy-done
  411.4 1.0 multiply_reduce_fusion.3
  412.4 44.7 %all-gather.17.cloned.1.call-done = bf16[2048,2048]{1,0:T(8,128)(2,1)} async-done(((bf16[256,2048]{1,0:T(8,128)(2,1)}), bf16[2048,2048]{1,0:T(8,128)(2,1)}) %all-gather.17.cloned.1.call-update) | async-done | bytes 8388624 | tf_op jit(solution)/shard_map/all_gather | solution.py:54
  457.1 16.0 fusion.48
  473.1 41.7 %all-gather.19.cloned.1.call-done = bf16[2048,2048]{1,0:T(8,128)(2,1)} async-done(((bf16[2048,256]{1,0:T(8,128)(2,1)}), bf16[2048,2048]{1,0:T(8,128)(2,1)}) %all-gather.19.cloned.1.call-update) | async-done | bytes 8388624 | tf_op jit(solution)/shard_map/all_gather | solution.py:55
  514.7 20.5 %fusion.58 = (f32[2048]{0:T(1024)}, bf16[1024,2048]{1,0:T(8,128)(2,1)S(1)}) fusion(f32[1024,2048]{1,0:T(8,128)} %fusion.48, f32[2048]{0:T(1024)S(1)} %bitcast.123, bf16[2048,2048]{1,0:T(8,128)(2,1)} %all-gather.19.cloned.1.call-done, bf16[1024,2048]{1,0:T(8,128)(2,1)} %param.16, pred[1024]{0:T(1024)(128)(4,1)S(1)} %iota_compare_fusion.1), kind=kOutput, calls=%fused_computation.107 | convolution fusion | flops 8642361344 | bytes 25183232 | tf_op jit(solution)/shard_map/sd,fd->sf/dot_general | solution.py:123
  535.2 1.9 copy-done.43
  537.2 13.2 fusion.27
  551.9 16.9 %convolution_convert_fusion = bf16[1024,2048]{1,0:T(8,128)(2,1)} fusion(bf16[2048,2048]{1,0:T(8,128)(2,1)} %all-gather.19.cloned.1.call-done, f32[1024,2048]{1,0:T(8,128)} %fusion.48, f32[2048]{0:T(1024)S(1)} %bitcast.124), kind=kOutput, calls=%fused_computation.53 | convolution fusion | flops 8613003264 | bytes 20979712 | tf_op jit(solution)/shard_map/dot_general | solution.py:107
  568.8 272.7 %all-reduce.15.cloned.1.call-done = f32[1024,2048]{1,0:T(8,128)} async-done(((f32[1024,2048]{1,0:T(8,128)}), f32[1024,2048]{1,0:T(8,128)}) %all-reduce.15.cloned.1.call-update) | async-done | bytes 8388624 | tf_op jit(solution)/shard_map/psum | solution.py:133
  841.4 8.0 multiply_reduce_fusion.1
  849.7 4.9 fusion.51
  854.6 6.7 fusion.34
  861.4 2.9 bitcast_convert_fusion.1
  864.3 10.6 multiply_reduce_fusion
  874.9 12.4 multiply_convert_fusion
  887.4 3.9 multiply_convert_fusion.2
  891.2 3.0 bitcast_convert_fusion.2
  894.3 1.3 copy.89
  895.8 1.6 copy.87
  897.4 1.5 copy.88
  898.9 2.2 bitcast_reduce_fusion.1
  901.1 0.9 copy.103
  902.1 11.0 bitcast_convert_fusion
  913.2 1.1 copy-done.15
  914.3 9.2 convolution_multiply_fusion.2
  923.6 17.6 %convolution_multiply_fusion = f32[2048,2048]{1,0:T(8,128)} fusion(f32[]{:T(128)S(6)} %div.63, bf16[1024,2048]{1,0:T(8,128)(2,1)} %param.16, pred[1024]{0:T(1024)(128)(4,1)S(1)} %iota_compare_fusion.1, f32[1024,2048]{1,0:T(8,128)} %fusion.48, f32[2048]{0:T(1024)S(1)} %bitcast.125), kind=kOutput, calls=%fused_computation.23 | convolution fusion | flops 8621391872 | bytes 29369348 | tf_op jit(solution)/shard_map/sf,sd->fd/dot_general | solution.py:119
  941.9 17.1 %convolution_multiply_fusion.1 = f32[2048,2048]{1,0:T(8,128)} fusion(f32[]{:T(128)S(6)} %div.63, bf16[1024,2048]{1,0:T(8,128)(2,1)} %copy-done.43, f32[1024,2048]{1,0:T(8,128)} %copy-done, f32[2048]{0:T(1024)S(1)} %bitcast.122, f32[2048]{0:T(1024)S(1)} %bitcast.98, f32[1024]{0:T(1024)S(1)} %fusion.42, f32[1024]{0:T(1024)S(1)} %broadcast_multiply_fusion.4), kind=kOutput, calls=%fused_computation.24 | convolution fusion | flops 8604614656 | bytes 29384708 | tf_op jit(solution)/shard_map/sd,sf->df/dot_general | solution.py:129
  959.1 1.2 copy-done.18
  960.3 13.7 broadcast_multiply_fusion
  974.6 8.9 all-gather.7
  984.8 1.4 copy.104
  986.2 242.6 %all-reduce.17.cloned.1.call-done = (bf16[1024,2048]{1,0:T(8,128)(2,1)}, bf16[1024,2048]{1,0:T(8,128)(2,1)}) async-done(((bf16[1024,2048]{1,0:T(8,128)(2,1)}, bf16[1024,2048]{1,0:T(8,128)(2,1)}), (bf16[1024,2048]{1,0:T(8,128)(2,1)}, bf16[1024,2048]{1,0:T(8,128)(2,1)})) %all-reduce.17.cloned.1.call-update) | async-done | bytes 8388624 | tf_op jit(solution)/shard_map/psum | solution.py:109
  1228.9 5.6 convert_reduce_fusion
  1234.8 4.4 fusion.18
  1239.3 10.4 fusion.19
  1249.8 25.4 %all-reduce.7 = (f32[2048]{0:T(1024)S(1)}, f32[2048]{0:T(1024)S(1)}, f32[2048]{0:T(1024)S(1)}, f32[2048]{0:T(1024)S(1)}, f32[2048]{0:T(1024)S(1)}, /*index=5*/f32[2048]{0:T(1024)S(1)}, f32[2048]{0:T(1024)S(1)}) all-reduce(f32[2048]{0:T(1024)S(1)} %bitcast.111, f32[2048]{0:T(1024)S(1)} %bitcast.110, ...), channel_id=6, replica_groups=mesh['dp'=8,'mp'=4] {'dp'}, use_global_device_ids=true, to_apply=%region_26.27.clone | all-reduce | flops 14336 | bytes 114688
  1279.7 8.5 add_convert_fusion
  1288.2 115.5 %reduce-scatter.14.cloned.1.call-done = f32[2048,256]{1,0:T(8,128)} async-done(((f32[2048,2048]{1,0:T(8,128)}), f32[2048,256]{1,0:T(8,128)}) %reduce-scatter.14.cloned.1.call-update) | async-done | bytes 2097168 | tf_op jit(solution)/shard_map/reduce_scatter | solution.py:190
  1403.7 120.4 %reduce-scatter.12.cloned.1.call-done = f32[256,2048]{1,0:T(8,128)} async-done(((f32[2048,2048]{1,0:T(8,128)}), f32[256,2048]{1,0:T(8,128)}) %reduce-scatter.12.cloned.1.call-update) | async-done | bytes 2097168 | tf_op jit(solution)/shard_map/reduce_scatter | solution.py:189
  1524.0 96.0 %reduce-scatter.8.cloned.1.call-done = f32[256,3,512]{2,0,1:T(8,128)} async-done(((f32[2048,3,512]{2,0,1:T(8,128)}), f32[256,3,512]{2,0,1:T(8,128)}) %reduce-scatter.8.cloned.1.call-update) | async-done | bytes 1572880 | tf_op jit(solution)/shard_map/reduce_scatter | solution.py:183
  (159 shorter events, 12.3 us)
Async XLA Ops:
  7.2 52.6 %all-gather.13.cloned.1.call-start = ((), (), s32[]{:S(2)}) async-start(), calls=%async_computation.5 | async-start | bytes 7077888 | tf_op jit(solution)/shard_map/all_gather | solution.py:52
  9.5 93.5 %all-gather.15.cloned.1.call-start = ((), (), s32[]{:S(2)}) async-start(), calls=%async_computation.6 | async-start | bytes 2359296 | tf_op jit(solution)/shard_map/all_gather | solution.py:53
  10.3 391.8 %all-reduce.13.cloned.1.call-start = ((), (), s32[]{:S(2)}) async-start(), calls=%async_computation.7 | async-start | bytes 16777216 | tf_op jit(solution)/shard_map/psum | solution.py:103
  22.4 49.7 %copy-start.29 = (f32[1,512]{1,0:T(1,128)}, f32[1,512]{1,0:T(1,128)S(1)}, u32[]{:S(2)}) copy-start(f32[1,512]{1,0:T(1,128)S(1)} %get-tuple-element.47) | copy-start | bytes 6148
  25.3 44.9 %copy-start.21 = (f32[1024]{0:T(1024)}, f32[1024]{0:T(1024)S(1)}, u32[]{:S(2)}) copy-start(f32[1024]{0:T(1024)S(1)} %broadcast_multiply_fusion.5) | copy-start | bytes 12292
  28.8 8.9 copy-start.25
  28.8 41.5 %copy-start.23 = (f32[1024]{0:T(1024)}, f32[1024]{0:T(1024)S(1)}, u32[]{:S(2)}) copy-start(f32[1024]{0:T(1024)S(1)} %fusion.41) | copy-start | bytes 12292
  37.7 32.6 %copy-start.31 = (f32[8,1,256]{2,1,0:T(1,128)}, f32[8,1,256]{2,1,0:T(1,128)S(1)}, u32[]{:S(2)}) copy-start(f32[8,1,256]{2,1,0:T(1,128)S(1)} %convert_element_type.130) | copy-start | bytes 24580
  46.3 23.9 %copy-start.19 = (f32[8,1,256]{2,1,0:T(1,128)}, f32[8,1,256]{2,1,0:T(1,128)S(1)}, u32[]{:S(2)}) copy-start(f32[8,1,256]{2,1,0:T(1,128)S(1)} %convert_element_type.129) | copy-start | bytes 24580
  70.4 9.3 copy-start.10
  72.1 7.7 copy-start.6
  89.9 8.5 copy-start.8
  98.4 3.2 copy-start.2
  103.0 7.8 copy-start.14
  110.8 1.3 copy-start.37
  110.8 1.3 copy-start.38
  110.8 1.3 copy-start.39
  110.8 1.3 copy-start.40
  110.8 35.4 %copy-start.36 = (s32[8]{0:T(128)S(1)}, s32[8]{0:T(128)}, u32[]{:S(2)}) copy-start(s32[8]{0:T(128)} %param.17) | copy-start | bytes 100
  110.9 346.2 %all-gather.17.cloned.1.call-start = ((), (), s32[]{:S(2)}) async-start(), calls=%async_computation.8 | async-start | bytes 9437184 | tf_op jit(solution)/shard_map/all_gather | solution.py:54
  111.5 403.3 %all-gather.19.cloned.1.call-start = ((), (), s32[]{:S(2)}) async-start(), calls=%async_computation.9 | async-start | bytes 9437184 | tf_op jit(solution)/shard_map/all_gather | solution.py:55
  112.0 729.4 %all-reduce.15.cloned.1.call-start = ((), (), s32[]{:S(2)}) async-start(), calls=%async_computation.10 | async-start | bytes 16777216 | tf_op jit(solution)/shard_map/psum | solution.py:133
  138.2 318.9 %copy-start.34 = (f32[8,1,256]{2,1,0:T(1,128)}, f32[8,1,256]{2,1,0:T(1,128)S(1)}, u32[]{:S(2)}) copy-start(f32[8,1,256]{2,1,0:T(1,128)S(1)} %convert_element_type.134) | copy-start | bytes 24580
  407.8 3.6 copy-start
  535.2 1.9 copy-start.43
  550.5 434.4 %reduce-scatter.16.cloned.1.call-start = ((), (), s32[]{:S(2)}) async-start(), calls=%async_computation.15 | async-start | bytes 294912
  841.4 8.2 copy-start.5
  849.7 5.0 copy-start.12
  849.7 11.7 slice-start
  854.6 6.7 copy-start.4
  854.6 6.7 slice-start.1
  861.3 3.0 copy-start.9
  874.9 12.4 copy-start.7
  874.9 12.4 copy-start.30
  887.3 3.9 copy-start.11
  895.6 6.5 copy-start.16
  898.9 3.2 copy-start.17
  902.0 326.9 %all-reduce.17.cloned.1.call-start = ((), (), s32[]{:S(2)}) async-start(), calls=%async_computation.16 | async-start | bytes 16777216 | tf_op jit(solution)/shard_map/psum | solution.py:109
  913.1 1.2 copy-start.15
  913.1 375.1 %reduce-scatter.10.cloned.1.call-start = ((), (), s32[]{:S(2)}) async-start(), calls=%async_computation.12 | async-start | bytes 4718592 | tf_op jit(solution)/shard_map/reduce_scatter | solution.py:184
  923.5 480.1 %reduce-scatter.14.cloned.1.call-start = ((), (), s32[]{:S(2)}) async-start(), calls=%async_computation.14 | async-start | bytes 18874368 | tf_op jit(solution)/shard_map/reduce_scatter | solution.py:190
  941.2 0.7 copy-start.35
  941.2 582.8 %reduce-scatter.12.cloned.1.call-start = ((), (), s32[]{:S(2)}) async-start(), calls=%async_computation.13 | async-start | bytes 18874368 | tf_op jit(solution)/shard_map/reduce_scatter | solution.py:189
  959.0 1.3 copy-start.18
  959.0 1.3 copy-start.20
  959.0 1.3 copy-start.22
  959.0 1.3 copy-start.24
  959.0 1.2 copy-start.32
  959.0 661.0 %reduce-scatter.8.cloned.1.call-start = ((), (), s32[]{:S(2)}) async-start(), calls=%async_computation.11 | async-start | bytes 14155776 | tf_op jit(solution)/shard_map/reduce_scatter | solution.py:183
  974.0 0.7 copy-start.41
  974.0 9.6 copy-start.42
  974.0 10.8 copy-start.33
  974.0 260.5 %copy-start.26 = (f32[1024]{0:T(1024)S(1)}, f32[1024]{0:T(1024)}, u32[]{:S(2)}) copy-start(f32[1024]{0:T(1024)} %copy-done.25) | copy-start | bytes 12292
  1228.9 5.6 copy-start.1
  1228.9 5.9 copy-start.3
  1228.9 10.4 copy-start.13
  1239.2 10.4 copy-start.27
  1239.2 10.4 copy-start.28
Sparse Core Ops, SparseCore 0:
  10.4 49.3 all-gather.12
  61.7 28.0 all-gather.14
  111.0 291.0 all-reduce.12
  403.8 53.2 all-gather.16
  458.8 55.8 all-gather.18
  550.6 290.8 all-reduce.14
  902.1 32.6 reduce-scatter.15
  938.0 290.8 all-reduce.16
  1232.8 50.8 reduce-scatter.9
  1287.7 115.9 reduce-scatter.13
  1407.8 116.1 reduce-scatter.11
  1527.9 92.0 reduce-scatter.7
where the time goes:
time: 1630 us
  waiting for transfers between devices  1200 us (74%)
  matrix products  190 us (12%)
  blocking collectives  96.2 us (6%)
  other arithmetic  87.9 us (5%)
  local copies, waits for them, and re-layouts  32.2 us (2%)
  between operations  17.2 us (1%)
    psum x1, waiting for transfers between devices, shards(): delta_two = lax.psum(two_part, 'mp')  273 us
    psum x1, waiting for transfers between devices, shards(): residual = inputs + lax.psum(attn_part, 'mp') + bias_out  255 us
    psum x1, waiting for transfers between devices, shards(): lax.psum(ffn_part.astype(jnp.bfloat16), 'mp').astype(jnp.float32)  243 us
    reduce_scatter x1, waiting for transfers between devices, shards(): lax.psum_scatter(grad_fc1, 'dp', scatter_dimension=0, tiled=True)  120 us
    reduce_scatter x1, waiting for transfers between devices, shards(): lax.psum_scatter(grad_fc2, 'dp', scatter_dimension=1, tiled=True)  115 us
    reduce_scatter x1, waiting for transfers between devices, shards(): lax.psum_scatter(grad_qkv, 'dp', scatter_dimension=0, tiled=True)  96 us
    all_gather x1, waiting for transfers between devices, shards(): lax.all_gather(w_fc1, 'dp', axis=0, tiled=True)  44.7 us
    all_gather x1, waiting for transfers between devices, shards(): lax.all_gather(w_fc2, 'dp', axis=1, tiled=True)  41.7 us
  transfers between devices with their start and end apart: 12, of which 9 were waited for; matrix products, arithmetic and copies ran while one was open for 12% of the time, Pallas kernels for 0%

commit v1 on v0

--- a/solution.py
+++ b/solution.py
@@ -48,10 +48,35 @@
     fc1_bias,
     fc2_bias,
 ):
+
+    def try_all_shifts_all(here_x, lane_axis):
+        m_next = lax.psum(1, lane_axis)
+        work_now, prior, carry_in = (m_next, lax.axis_index(lane_axis), here_x.shape[0])
+        z1 = map(lambda dd: (dd, (dd + 1) % work_now), range(work_now))
+        pile = list(z1)
+        copies = list(map(lambda dd: (dd, (dd - 1) % work_now), range(work_now)))
+        u_next = jnp.zeros(
+            (*here_x.shape[:0], work_now * carry_in, *here_x.shape[1:]), here_x.dtype
+        )
+        u_next = lax.dynamic_update_slice_in_dim(u_next, here_x, prior * carry_in, axis=0)
+        response = front = here_x
+        block_now = work_now // 2
+        for dev in range(1, block_now + 1):
+            response = lax.ppermute(response, lane_axis, pile)
+            u_next = lax.dynamic_update_slice_in_dim(
+                u_next, response, (prior - dev) % work_now * carry_in, axis=0
+            )
+            if dev < work_now - block_now:
+                front = lax.ppermute(front, lane_axis, copies)
+                u_next = lax.dynamic_update_slice_in_dim(
+                    u_next, front, (prior + dev) % work_now * carry_in, axis=0
+                )
+        return u_next
+
     gathered = (
         lax.all_gather(w_qkv, "dp", axis=0, tiled=True),
         lax.all_gather(w_out, "dp", axis=1, tiled=True),
-        lax.all_gather(w_fc1, "dp", axis=0, tiled=True),
+        try_all_shifts_all(w_fc1, "dp"),
         lax.all_gather(w_fc2, "dp", axis=1, tiled=True),
         lax.all_gather(ln1_gain, "dp", axis=0, tiled=True),
         lax.all_gather(ln1_bias, "dp", axis=0, tiled=True),

time: 1630 us -> 1580 us (0.969)
  waiting for transfers between devices: 1200 us -> 1120 us
    psum x1, waiting for transfers between devices: 255 us -> 163 us  [shards(): residual = inputs + lax.psum(attn_part, 'mp') + bias_out]
    ppermute x0 -> x7, waiting for transfers between devices: none -> 62.8 us  [the longest x4 47.7 us: try_all_shifts_all(): response = lax.ppermute(response, lane_axis, pile)]
    all_gather x1 -> x0, waiting for transfers between devices: 44.7 us -> none  [shards(): lax.all_gather(w_fc1, 'dp', axis=0, tiled=True)]
  transfers between devices with their start and end apart: 12 -> 18, of which waited for: 9 -> 12; matrix products, arithmetic and copies ran while one was open for 12% -> 13% of each run, Pallas kernels for 0% -> 0%
where the time goes in v1:
time: 1580 us; the launch traced here: 1570 us
  waiting for transfers between devices  1120 us (71%)
  matrix products  187 us (12%)
  blocking collectives  104 us (7%)
  other arithmetic  87.7 us (6%)
  local copies, waits for them, and re-layouts  46.8 us (3%)
  between operations  16.9 us (1%)
    psum x1, waiting for transfers between devices, shards(): delta_two = lax.psum(two_part, 'mp')  273 us
    psum x1, waiting for transfers between devices, shards(): lax.psum(ffn_part.astype(jnp.bfloat16), 'mp').astype(jnp.float32)  243 us
    psum x1, waiting for transfers between devices, shards(): residual = inputs + lax.psum(attn_part, 'mp') + bias_out  163 us
    reduce_scatter x1, waiting for transfers between devices, shards(): lax.psum_scatter(grad_fc1, 'dp', scatter_dimension=0, tiled=True)  120 us
    reduce_scatter x1, waiting for transfers between devices, shards(): lax.psum_scatter(grad_fc2, 'dp', scatter_dimension=1, tiled=True)  116 us
    reduce_scatter x1, waiting for transfers between devices, shards(): lax.psum_scatter(grad_qkv, 'dp', scatter_dimension=0, tiled=True)  96.2 us
    ppermute x4, waiting for transfers between devices, try_all_shifts_all(): response = lax.ppermute(response, lane_axis, pile)  47.7 us
    all_gather x1, waiting for transfers between devices, shards(): lax.all_gather(w_fc2, 'dp', axis=1, tiled=True)  33.6 us
  transfers between devices with their start and end apart: 18, of which 12 were waited for; matrix products, arithmetic and copies ran while one was open for 13% of the time, Pallas kernels for 0%

profile of v1, /device:TPU:0, one launch (start us, length us, event | category | flops | bytes accessed | tf_op | source)
XLA Modules:
  0.0 1571.2 jit_solution(14756623118205757407)
XLA Ops:
  7.2 2.3 copy.76
  12.0 10.4 all-gather.2
  22.4 2.9 convert_reduce_fusion.1
  25.3 3.4 fusion.15
  28.8 8.9 all-gather.1
  37.7 8.6 all-gather
  46.3 13.5 all-gather.12.cloned.1.call-done
  59.8 10.4 fusion.38
  70.4 1.7 fusion.54
  72.1 7.7 fusion.57
  79.8 8.1 fusion
  87.9 2.0 copy.78
  89.9 8.5 divide_convert_fusion
  98.4 3.2 copy-done.2
  103.2 7.8 fusion.59
  111.8 2.5 collective-permute-start.1
  114.3 22.6 %collective-permute-done = bf16[256,2048]{1,0:T(8,128)(2,1)S(1)} collective-permute-done((bf16[256,2048]{1,0:T(8,128)(2,1)S(1)}, bf16[256,2048]{1,0:T(8,128)(2,1)S(1)}, u32[]{:S(2)}, u32[]{:S(2)}) %collective-permute-start) | collective-permute-done | bytes 1048608 | tf_op jit(solution)/shard_map/ppermute | solution.py:65
  136.9 2.6 collective-permute-start.3
  139.6 23.2 %collective-permute-done.2 = bf16[256,2048]{1,0:T(8,128)(2,1)} collective-permute-done((bf16[256,2048]{1,0:T(8,128)(2,1)S(1)}, bf16[256,2048]{1,0:T(8,128)(2,1)}, u32[]{:S(2)}, u32[]{:S(2)}) %collective-permute-start.2) | collective-permute-done | bytes 1048608 | tf_op jit(solution)/shard_map/ppermute | solution.py:65
  162.8 16.0 %all-gather.6 = bf16[8,1,256]{2,1,0:T(2,128)(2,1)S(1)} all-gather(bf16[1,1,256]{2,1,0:T(2,128)(2,1)S(1)} %reshape.172), channel_id=1, replica_groups=mesh['dp'=8,'mp'=4] {'dp'}, dimensions={0}, use_global_device_ids=true | all-gather | bytes 4608 | tf_op jit(solution)/shard_map/all_gather | solution.py:87
  178.9 8.5 all-gather.3
  187.4 9.3 all-gather.5
  196.7 7.8 all-gather.4
  205.8 4.3 broadcast_in_dim.44
  214.7 2.3 constant_dynamic-update-slice_fusion.4
  217.1 2.3 constant_dynamic-update-slice_fusion.3
  220.5 15.1 collective-permute-done.5
  236.6 1.9 collective-permute-done.6
  239.6 162.6 %all-reduce.13.cloned.1.call-done = f32[1024,2048]{1,0:T(8,128)} async-done(((f32[1024,2048]{1,0:T(8,128)}), f32[1024,2048]{1,0:T(8,128)}) %all-reduce.13.cloned.1.call-update) | async-done | bytes 8388624 | tf_op jit(solution)/shard_map/psum | solution.py:128
  402.2 5.7 fusion.52
  408.9 2.6 copy-done
  411.5 13.7 fusion.48
  425.1 33.6 %all-gather.16.cloned.1.call-done = bf16[2048,2048]{1,0:T(8,128)(2,1)} async-done(((bf16[2048,256]{1,0:T(8,128)(2,1)}), bf16[2048,2048]{1,0:T(8,128)(2,1)}) %all-gather.16.cloned.1.call-update) | async-done | bytes 8388624 | tf_op jit(solution)/shard_map/all_gather | solution.py:80
  458.8 20.5 %fusion.58 = (f32[2048]{0:T(1024)}, bf16[1024,2048]{1,0:T(8,128)(2,1)S(1)}) fusion(f32[1024,2048]{1,0:T(8,128)} %fusion.48, f32[2048]{0:T(1024)S(1)} %bitcast.123, bf16[2048,2048]{1,0:T(8,128)(2,1)} %all-gather.16.cloned.1.call-done, bf16[1024,2048]{1,0:T(8,128)(2,1)} %param.16, pred[1024]{0:T(1024)(128)(4,1)S(1)} %iota_compare_fusion.1), kind=kOutput, calls=%fused_computation.115 | convolution fusion | flops 8642361344 | bytes 25183232 | tf_op jit(solution)/shard_map/sd,fd->sf/dot_general | solution.py:148
  479.3 1.9 copy-done.46
  481.3 13.3 fusion.27
  496.0 16.9 %convolution_convert_fusion = bf16[1024,2048]{1,0:T(8,128)(2,1)} fusion(bf16[2048,2048]{1,0:T(8,128)(2,1)} %all-gather.16.cloned.1.call-done, f32[1024,2048]{1,0:T(8,128)} %fusion.48, f32[2048]{0:T(1024)S(1)} %bitcast.124), kind=kOutput, calls=%fused_computation.53 | convolution fusion | flops 8613003264 | bytes 20979712 | tf_op jit(solution)/shard_map/dot_general | solution.py:132
  512.9 272.7 %all-reduce.15.cloned.1.call-done = f32[1024,2048]{1,0:T(8,128)} async-done(((f32[1024,2048]{1,0:T(8,128)}), f32[1024,2048]{1,0:T(8,128)}) %all-reduce.15.cloned.1.call-update) | async-done | bytes 8388624 | tf_op jit(solution)/shard_map/psum | solution.py:158
  785.6 8.0 multiply_reduce_fusion.1
  793.8 4.9 fusion.51
  798.8 6.7 fusion.34
  805.5 2.9 bitcast_convert_fusion.1
  808.5 10.6 multiply_reduce_fusion
  819.1 12.4 multiply_convert_fusion
  831.5 3.9 multiply_convert_fusion.2
  835.4 3.0 bitcast_convert_fusion.2
  839.9 1.6 copy.87
  841.5 1.5 copy.88
  843.0 2.2 bitcast_reduce_fusion.1
  846.2 11.0 bitcast_convert_fusion
  858.5 9.2 convolution_multiply_fusion.2
  867.7 17.6 %convolution_multiply_fusion = f32[2048,2048]{1,0:T(8,128)} fusion(f32[]{:T(128)S(6)} %div.63, bf16[1024,2048]{1,0:T(8,128)(2,1)} %param.16, pred[1024]{0:T(1024)(128)(4,1)S(1)} %iota_compare_fusion.1, f32[1024,2048]{1,0:T(8,128)} %fusion.48, f32[2048]{0:T(1024)S(1)} %bitcast.125), kind=kOutput, calls=%fused_computation.23 | convolution fusion | flops 8621391872 | bytes 29369348 | tf_op jit(solution)/shard_map/sf,sd->fd/dot_general | solution.py:144
  886.0 17.1 %convolution_multiply_fusion.1 = f32[2048,2048]{1,0:T(8,128)} fusion(f32[]{:T(128)S(6)} %div.63, bf16[1024,2048]{1,0:T(8,128)(2,1)} %copy-done.46, f32[1024,2048]{1,0:T(8,128)} %copy-done, f32[2048]{0:T(1024)S(1)} %bitcast.122, f32[2048]{0:T(1024)S(1)} %bitcast.98, f32[1024]{0:T(1024)S(1)} %fusion.42, f32[1024]{0:T(1024)S(1)} %broadcast_multiply_fusion.4), kind=kOutput, calls=%fused_computation.24 | convolution fusion | flops 8604614656 | bytes 29384708 | tf_op jit(solution)/shard_map/sd,sf->df/dot_general | solution.py:154
  904.4 13.7 broadcast_multiply_fusion
  918.8 8.9 all-gather.7
  930.4 242.6 %all-reduce.17.cloned.1.call-done = (bf16[1024,2048]{1,0:T(8,128)(2,1)}, bf16[1024,2048]{1,0:T(8,128)(2,1)}) async-done(((bf16[1024,2048]{1,0:T(8,128)(2,1)}, bf16[1024,2048]{1,0:T(8,128)(2,1)}), (bf16[1024,2048]{1,0:T(8,128)(2,1)}, bf16[1024,2048]{1,0:T(8,128)(2,1)})) %all-reduce.17.cloned.1.call-update) | async-done | bytes 8388624 | tf_op jit(solution)/shard_map/psum | solution.py:134
  1173.1 5.4 convert_reduce_fusion
  1179.0 4.4 fusion.18
  1183.4 10.4 fusion.19
  1194.0 25.5 %all-reduce.7 = (f32[2048]{0:T(1024)S(1)}, f32[2048]{0:T(1024)S(1)}, f32[2048]{0:T(1024)S(1)}, f32[2048]{0:T(1024)S(1)}, f32[2048]{0:T(1024)S(1)}, /*index=5*/f32[2048]{0:T(1024)S(1)}, f32[2048]{0:T(1024)S(1)}) all-reduce(f32[2048]{0:T(1024)S(1)} %bitcast.111, f32[2048]{0:T(1024)S(1)} %bitcast.110, ...), channel_id=6, replica_groups=mesh['dp'=8,'mp'=4] {'dp'}, use_global_device_ids=true, to_apply=%region_26.27.clone | all-reduce | flops 14336 | bytes 114688
  1223.9 8.5 add_convert_fusion
  1232.4 115.7 %reduce-scatter.14.cloned.1.call-done = f32[2048,256]{1,0:T(8,128)} async-done(((f32[2048,2048]{1,0:T(8,128)}), f32[2048,256]{1,0:T(8,128)}) %reduce-scatter.14.cloned.1.call-update) | async-done | bytes 2097168 | tf_op jit(solution)/shard_map/reduce_scatter | solution.py:215
  1348.0 120.2 %reduce-scatter.12.cloned.1.call-done = f32[256,2048]{1,0:T(8,128)} async-done(((f32[2048,2048]{1,0:T(8,128)}), f32[256,2048]{1,0:T(8,128)}) %reduce-scatter.12.cloned.1.call-update) | async-done | bytes 2097168 | tf_op jit(solution)/shard_map/reduce_scatter | solution.py:214
  1468.2 96.2 %reduce-scatter.8.cloned.1.call-done = f32[256,3,512]{2,0,1:T(8,128)} async-done(((f32[2048,3,512]{2,0,1:T(8,128)}), f32[256,3,512]{2,0,1:T(8,128)}) %reduce-scatter.8.cloned.1.call-update) | async-done | bytes 1572880 | tf_op jit(solution)/shard_map/reduce_scatter | solution.py:208
  (185 shorter events, 28.8 us)
Async XLA Ops:
  7.2 52.6 %all-gather.12.cloned.1.call-start = ((), (), s32[]{:S(2)}) async-start(), calls=%async_computation.5 | async-start | bytes 7077888 | tf_op jit(solution)/shard_map/all_gather | solution.py:77
  9.5 93.6 %all-gather.14.cloned.1.call-start = ((), (), s32[]{:S(2)}) async-start(), calls=%async_computation.6 | async-start | bytes 2359296 | tf_op jit(solution)/shard_map/all_gather | solution.py:78
  10.3 391.9 %all-reduce.13.cloned.1.call-start = ((), (), s32[]{:S(2)}) async-start(), calls=%async_computation.7 | async-start | bytes 16777216 | tf_op jit(solution)/shard_map/psum | solution.py:128
  22.4 49.7 %copy-start.32 = (f32[1,512]{1,0:T(1,128)}, f32[1,512]{1,0:T(1,128)S(1)}, u32[]{:S(2)}) copy-start(f32[1,512]{1,0:T(1,128)S(1)} %get-tuple-element.47) | copy-start | bytes 6148
  25.3 44.9 %copy-start.24 = (f32[1024]{0:T(1024)}, f32[1024]{0:T(1024)S(1)}, u32[]{:S(2)}) copy-start(f32[1024]{0:T(1024)S(1)} %broadcast_multiply_fusion.5) | copy-start | bytes 12292
  28.8 8.9 copy-start.28
  28.8 41.5 %copy-start.26 = (f32[1024]{0:T(1024)}, f32[1024]{0:T(1024)S(1)}, u32[]{:S(2)}) copy-start(f32[1024]{0:T(1024)S(1)} %fusion.41) | copy-start | bytes 12292
  37.7 32.6 %copy-start.34 = (f32[8,1,256]{2,1,0:T(1,128)}, f32[8,1,256]{2,1,0:T(1,128)S(1)}, u32[]{:S(2)}) copy-start(f32[8,1,256]{2,1,0:T(1,128)S(1)} %convert_element_type.130) | copy-start | bytes 24580
  46.3 23.9 %copy-start.22 = (f32[8,1,256]{2,1,0:T(1,128)}, f32[8,1,256]{2,1,0:T(1,128)S(1)}, u32[]{:S(2)}) copy-start(f32[8,1,256]{2,1,0:T(1,128)S(1)} %convert_element_type.129) | copy-start | bytes 24580
  70.4 9.3 copy-start.10
  72.1 7.7 copy-start.6
  89.9 8.5 copy-start.8
  98.4 3.2 copy-start.2
  103.1 7.9 copy-start.14
  103.1 8.5 copy-start.16
  103.1 59.7 %copy-start.40 = (bf16[256]{0:T(256)(128)(2,1)S(1)}, bf16[256]{0:T(256)(128)(2,1)}, u32[]{:S(2)}) copy-start(bf16[256]{0:T(256)(128)(2,1)} %param.24) | copy-start | bytes 1540
  103.1 59.6 %copy-start.41 = (bf16[256]{0:T(256)(128)(2,1)S(1)}, bf16[256]{0:T(256)(128)(2,1)}, u32[]{:S(2)}) copy-start(bf16[256]{0:T(256)(128)(2,1)} %param.25) | copy-start | bytes 1540
  103.1 59.7 %copy-start.42 = (bf16[256]{0:T(256)(128)(2,1)S(1)}, bf16[256]{0:T(256)(128)(2,1)}, u32[]{:S(2)}) copy-start(bf16[256]{0:T(256)(128)(2,1)} %param.27) | copy-start | bytes 1540
  103.1 59.7 %copy-start.43 = (bf16[256]{0:T(256)(128)(2,1)S(1)}, bf16[256]{0:T(256)(128)(2,1)}, u32[]{:S(2)}) copy-start(bf16[256]{0:T(256)(128)(2,1)} %param.28) | copy-start | bytes 1540
  103.2 101.3 %copy-start.39 = (s32[8]{0:T(128)S(1)}, s32[8]{0:T(128)}, u32[]{:S(2)}) copy-start(s32[8]{0:T(128)} %param.17) | copy-start | bytes 100
  111.0 347.8 %all-gather.16.cloned.1.call-start = ((), (), s32[]{:S(2)}) async-start(), calls=%async_computation.8 | async-start | bytes 9437184 | tf_op jit(solution)/shard_map/all_gather | solution.py:80
  111.5 674.0 %all-reduce.15.cloned.1.call-start = ((), (), s32[]{:S(2)}) async-start(), calls=%async_computation.9 | async-start | bytes 16777216 | tf_op jit(solution)/shard_map/psum | solution.py:158
  111.6 25.3 %collective-permute-start = (bf16[256,2048]{1,0:T(8,128)(2,1)S(1)}, bf16[256,2048]{1,0:T(8,128)(2,1)S(1)}, u32[]{:S(2)}, u32[]{:S(2)}) collective-permute-start(bf16[256,2048]{1,0:T(8,128)(2,1)S(1)} %copy-done.16), channel_id=1, source_target_pairs={{0,4},{4,8},{8,12},{12,16},{16,20},{20,24},{24,28},{28,0},{1,5},{5... | collective-permute-start | bytes 3145736 | tf_op jit(solution)/shard_map/ppermute | solution.py:65
  111.8 25.1 %collective-permute-start.1 = (bf16[256,2048]{1,0:T(8,128)(2,1)S(1)}, bf16[256,2048]{1,0:T(8,128)(2,1)S(1)}, u32[]{:S(2)}, u32[]{:S(2)}) collective-permute-start(bf16[256,2048]{1,0:T(8,128)(2,1)S(1)} %copy-done.16), channel_id=1, source_target_pairs={{0,28},{4,0},{8,4},{12,8},{16,12},{20,16},{24,20},{28,24},{1,29},{... | collective-permute-start | bytes 3145736 | tf_op jit(solution)/shard_map/ppermute | solution.py:70
  136.9 2.7 copy-start.17
  136.9 25.8 %collective-permute-start.2 = (bf16[256,2048]{1,0:T(8,128)(2,1)S(1)}, bf16[256,2048]{1,0:T(8,128)(2,1)}, u32[]{:S(2)}, u32[]{:S(2)}) collective-permute-start(bf16[256,2048]{1,0:T(8,128)(2,1)S(1)} %collective-permute-done), channel_id=1, source_target_pairs={{0,4},{4,8},{8,12},{12,16},{16,20},{20,24},{24,28},{28,0},{1,5},{5... | collective-permute-start | bytes 3145736 | tf_op jit(solution)/shard_map/ppermute | solution.py:65
  136.9 74.3 %collective-permute-start.3 = (bf16[256,2048]{1,0:T(8,128)(2,1)S(1)}, bf16[256,2048]{1,0:T(8,128)(2,1)}, u32[]{:S(2)}, u32[]{:S(2)}) collective-permute-start(bf16[256,2048]{1,0:T(8,128)(2,1)S(1)} %collective-permute-done.1), channel_id=1, source_target_pairs={{0,28},{4,0},{8,4},{12,8},{16,12},{20,16},{24,20},{28,24},{1,29},{... | collective-permute-start | bytes 3145736 | tf_op jit(solution)/shard_map/ppermute | solution.py:70
  162.8 50.9 %collective-permute-start.4 = (bf16[256,2048]{1,0:T(8,128)(2,1)}, bf16[256,2048]{1,0:T(8,128)(2,1)S(1)}, u32[]{:S(2)}, u32[]{:S(2)}) collective-permute-start(bf16[256,2048]{1,0:T(8,128)(2,1)} %collective-permute-done.2), channel_id=1, source_target_pairs={{0,4},{4,8},{8,12},{12,16},{16,20},{20,24},{24,28},{28,0},{1,5},{5... | collective-permute-start | bytes 3145736 | tf_op jit(solution)/shard_map/ppermute | solution.py:65
  196.7 212.2 %copy-start.36 = (f32[8,1,256]{2,1,0:T(1,128)}, f32[8,1,256]{2,1,0:T(1,128)S(1)}, u32[]{:S(2)}) copy-start(f32[8,1,256]{2,1,0:T(1,128)S(1)} %convert_element_type.134) | copy-start | bytes 24580
  204.5 8.1 copy-start.18
  211.2 24.4 %collective-permute-start.5 = (bf16[256,2048]{1,0:T(8,128)(2,1)}, bf16[256,2048]{1,0:T(8,128)(2,1)S(1)}, u32[]{:S(2)}, u32[]{:S(2)}) collective-permute-start(bf16[256,2048]{1,0:T(8,128)(2,1)} %collective-permute-done.3), channel_id=1, source_target_pairs={{0,28},{4,0},{8,4},{12,8},{16,12},{20,16},{24,20},{28,24},{1,29},{... | collective-permute-start | bytes 3145736 | tf_op jit(solution)/shard_map/ppermute | solution.py:70
  213.6 24.9 %collective-permute-start.6 = (bf16[256,2048]{1,0:T(8,128)(2,1)S(1)}, bf16[256,2048]{1,0:T(8,128)(2,1)S(1)}, u32[]{:S(2)}, u32[]{:S(2)}) collective-permute-start(bf16[256,2048]{1,0:T(8,128)(2,1)S(1)} %collective-permute-done.4), channel_id=1, source_target_pairs={{0,4},{4,8},{8,12},{12,16},{16,20},{20,24},{24,28},{28,0},{1,5},{5... | collective-permute-start | bytes 3145736 | tf_op jit(solution)/shard_map/ppermute | solution.py:65
  407.9 3.6 copy-start
  479.3 1.9 copy-start.46
  494.6 434.4 %reduce-scatter.16.cloned.1.call-start = ((), (), s32[]{:S(2)}) async-start(), calls=%async_computation.14 | async-start | bytes 294912
  785.6 8.2 copy-start.5
  793.8 5.0 copy-start.12
  793.8 11.7 slice-start
  798.8 6.7 copy-start.4
  798.8 6.7 slice-start.1
  805.5 3.0 copy-start.9
  819.1 12.4 copy-start.7
  819.1 12.4 copy-start.33
  831.5 3.9 copy-start.11
  839.7 6.5 copy-start.19
  843.0 3.2 copy-start.20
  846.1 326.9 %all-reduce.17.cloned.1.call-start = ((), (), s32[]{:S(2)}) async-start(), calls=%async_computation.15 | async-start | bytes 16777216 | tf_op jit(solution)/shard_map/psum | solution.py:134
  857.3 375.1 %reduce-scatter.10.cloned.1.call-start = ((), (), s32[]{:S(2)}) async-start(), calls=%async_computation.11 | async-start | bytes 4718592 | tf_op jit(solution)/shard_map/reduce_scatter | solution.py:209
  867.7 480.3 %reduce-scatter.14.cloned.1.call-start = ((), (), s32[]{:S(2)}) async-start(), calls=%async_computation.13 | async-start | bytes 18874368 | tf_op jit(solution)/shard_map/reduce_scatter | solution.py:215
  885.4 582.9 %reduce-scatter.12.cloned.1.call-start = ((), (), s32[]{:S(2)}) async-start(), calls=%async_computation.12 | async-start | bytes 18874368 | tf_op jit(solution)/shard_map/reduce_scatter | solution.py:214
  903.2 1.3 copy-start.21
  903.2 1.3 copy-start.23
  903.2 1.3 copy-start.25
  903.2 1.3 copy-start.27
  903.2 1.2 copy-start.35
  903.2 661.2 %reduce-scatter.8.cloned.1.call-start = ((), (), s32[]{:S(2)}) async-start(), calls=%async_computation.10 | async-start | bytes 14155776 | tf_op jit(solution)/shard_map/reduce_scatter | solution.py:208
  918.1 9.6 copy-start.45
  918.1 10.8 copy-start.38
  918.1 260.3 %copy-start.29 = (f32[1024]{0:T(1024)S(1)}, f32[1024]{0:T(1024)}, u32[]{:S(2)}) copy-start(f32[1024]{0:T(1024)} %copy-done.28) | copy-start | bytes 12292
  1173.1 5.5 copy-start.1
  1173.1 5.9 copy-start.3
  1173.1 10.4 copy-start.13
  1183.4 10.4 copy-start.30
  1183.4 10.4 copy-start.31
  (3 other events, 2.6 us)
Sparse Core Ops, SparseCore 0:
  10.4 49.3 all-gather.11
  61.7 28.0 all-gather.13
  111.1 291.0 all-reduce.12
  403.9 54.8 all-gather.15
  494.7 290.8 all-reduce.14
  846.3 32.6 reduce-scatter.15
  882.1 290.8 all-reduce.16
  1177.0 50.8 reduce-scatter.9
  1232.0 115.9 reduce-scatter.13
  1352.0 116.1 reduce-scatter.11
  1472.3 92.0 reduce-scatter.7
